TPU v7x, 8 devices: a whole 2x2x1 slice. The times are simulated.
8 devices in a mesh: data: 2 (over z, y), tp: 4 (over x, core).
Axes of the slice: x: 2, y: 2, z: 1, core: 2. Of those that a mesh axis runs over, the one named last changes fastest.
Arguments:
- x: bfloat16 [2048, 49152], P('data', 'tp'), parts along dimension 0
- w: bfloat16 [49152, 12288], P('tp')
- lengths: int32 [8], P('data'), parts along dimension 0
Outputs:
- output: bfloat16 [2048, 12288], P('data'), parts along dimension 0
There are 2 independent parts. A program takes and returns all parts, laid end to end along the dimension named above; an argument that names none is the same for every part.
All inputs are finite; a program needn't handle non-finite values.
Results may differ from a plain program's by a relative error of at most 0.001.
Values are sent between devices in bfloat16 or wider.
A program may use at most 1.5 GiB of HBM per device.

v0:
```python
import jax
import jax.numpy as jnp
from jax import lax
from jax.sharding import PartitionSpec as P


def solution(mesh):
    tp_size = mesh.shape["tp"]

    def local_part(x_loc, w_loc, lengths):
        tokens = x_loc.shape[0]
        seq_len = tokens // lengths.shape[0]
        rows_dev = tokens // tp_size
        part_sum = jnp.dot(x_loc, w_loc, preferred_element_type=jnp.float32)
        own_rows = lax.psum_scatter(part_sum, "tp", scatter_dimension=0, tiled=True)
        valid = (jnp.arange(seq_len, dtype=jnp.int32)[None, :] < lengths[:, None]).reshape(-1)
        own_valid = lax.dynamic_slice_in_dim(valid, lax.axis_index("tp") * rows_dev, rows_dev)
        own_out = jnp.where(own_valid[:, None], own_rows, 0.0).astype(jnp.bfloat16)
        return lax.all_gather(own_out, "tp", axis=0, tiled=True)

    return jax.shard_map(local_part, mesh=mesh, in_specs=(P("data", "tp"), P("tp", None), P("data")), out_specs=P("data", None), check_vma=False)
```

profile of v0, /device:TPU:0, one launch (start us, length us, event | category | flops | bytes accessed | tf_op | source)
XLA Modules:
  0.0 851.2 jit_solution(1493136398821680577)
XLA Ops:
  6.5 0.0 reduce-scatter.2.cloned.1.call-start
  6.5 326.3 %fusion = f32[1024,12288]{1,0:T(8,128)} fusion(bf16[1024,12288]{1,0:T(8,128)(2,1)} %param.3, bf16[12288,12288]{1,0:T(8,128)(2,1)} %param.4), kind=kOutput, calls=%fused_computation.2 | convolution fusion | flops 309237645312 | bytes 377487360 | tf_op jit(solution)/shard_map/dot_general | solution.py:14
  332.8 0.0 copy-start
  332.8 0.0 reduce-scatter.2.cloned.1.call-update
  332.8 0.0 all-gather.2.cloned.1.call-start
  332.9 0.6 copy-done
  333.5 0.1 iota_compare_fusion
  333.5 0.1 dynamic_slice.3
  333.6 328.3 %reduce-scatter.2.cloned.1.call-done = f32[256,12288]{1,0:T(8,128)} async-done(((f32[1024,12288]{1,0:T(8,128)}), f32[256,12288]{1,0:T(8,128)}) %reduce-scatter.2.cloned.1.call-update) | async-done | bytes 12582928 | tf_op jit(solution)/shard_map/reduce_scatter | solution.py:15
  661.9 8.6 %select_convert_fusion = bf16[256,12288]{1,0:T(8,128)(2,1)} fusion(f32[256,12288]{1,0:T(8,128)} %reduce-scatter.2.cloned.1.call-done, pred[256]{0:T(512)(128)(4,1)S(1)} %dynamic_slice.3), kind=kLoop, calls=%fused_computation | loop fusion | flops 3145728 | bytes 18874624 | tf_op jit(solution)/shard_map/convert_element_type | solution.py:18
  670.5 0.0 all-gather.2.cloned.1.call-update
  670.5 153.0 %all-gather.2.cloned.1.call-done = bf16[1024,12288]{1,0:T(8,128)(2,1)} async-done(((bf16[256,12288]{1,0:T(8,128)(2,1)}), bf16[1024,12288]{1,0:T(8,128)(2,1)}) %all-gather.2.cloned.1.call-update) | async-done | bytes 25165840 | tf_op jit(solution)/shard_map/all_gather | solution.py:19
  823.5 20.9 %copy.5 = bf16[1024,12288]{1,0:T(8,128)(2,1)} copy(bf16[1024,12288]{1,0:T(8,128)(2,1)} %all-gather.2.cloned.1.call-done) | data formatting | bytes 50331648
  (1 shorter events, 0.0 us)
Async XLA Ops:
  6.5 655.4 %reduce-scatter.2.cloned.1.call-start = ((), (), s32[]{:S(2)}) async-start(), calls=%async_computation.1 | async-start | bytes 62914560 | tf_op jit(solution)/shard_map/reduce_scatter | solution.py:15
  332.8 0.7 copy-start
  332.8 490.7 %all-gather.2.cloned.1.call-start = ((), (), s32[]{:S(2)}) async-start(), calls=%async_computation.2 | async-start | bytes 31457280 | tf_op jit(solution)/shard_map/all_gather | solution.py:19
Sparse Core Ops, SparseCore 0:
  333.0 328.9 reduce-scatter.1
  670.6 152.8 all-gather.1
where the time goes:
time: 851 us
  waiting for transfers between devices  481 us (57%)
  matrix products  326 us (38%)
  local copies, waits for them, and re-layouts  21.5 us (3%)
  between operations  13.4 us (2%)
  other arithmetic  8.64 us (1%)
    reduce_scatter x1, waiting for transfers between devices, local_part(): own_rows = lax.psum_scatter(part_sum, 'tp', scatter_dimension=0, tiled=True)  328 us
    dot_general x1, matrix products, local_part(): part_sum = jnp.dot(x_loc, w_loc, preferred_element_type=jnp.float32)  326 us
    all_gather x1, waiting for transfers between devices, local_part(): return lax.all_gather(own_out, 'tp', axis=0, tiled=True)  153 us
    unnamed x3, local copies, waits for them, and re-layouts  21.4 us
  transfers between devices with their start and end apart: 2, of which 2 were waited for; matrix products, arithmetic and copies ran while one was open for 0% of the time, Pallas kernels for 0%

commit v1 on v0

v1 whole, which is shorter than its diff:
```python
import functools

import jax
import jax.numpy as jnp
from jax import lax
from jax.experimental import pallas as pl
from jax.experimental.pallas import tpu as pltpu
from jax.sharding import PartitionSpec as P

MESH = pl.DeviceIdType.MESH
TILE = 16
NB = 256
HB = NB // 2
XC = 2048
KC = 6144
BUCKETS = (320, 384, 448, 512, 576, 640, 704, 784)
LAST = 7


def tile_offsets(lens_ref, slots):
    offs, total = [], 0
    for s in range(slots):
        offs.append(total)
        total = total + (lens_ref[s] + TILE - 1) // TILE
    return offs, total


def fused_kernel(rows, table_ref, x_ref, w_ref, y_ref, xp, stage0, stage1, wbuf, part, ra, sb, so, rb, out,
                 xsem, wsem, send_a, recv_a, send_b, recv_b, send_c, recv_c, send_e, recv_e, send_d, recv_d, osem):
    depth, cols = w_ref.shape
    blocks = cols // NB
    half = rows // 2
    stages = (stage0, stage1)
    me = lax.axis_index("tp")
    core = lax.rem(me, 2)
    chip = me // 2
    sibling = {"tp": me + 1 - 2 * core}
    peer = {"tp": lax.rem(me + 2, 4)}
    nx = depth // XC
    nk = depth // KC

    def x_copy(k):
        return pltpu.make_async_copy(x_ref.at[:, :, pl.ds(k * XC, XC)], stages[k % 2], xsem.at[k % 2])

    def w_copy(b):
        s = lax.rem(b, 2)
        return pltpu.make_async_copy(w_ref.at[:, pl.ds(pl.multiple_of(b * NB, NB), NB)], wbuf.at[s], wsem.at[s])

    def remote(src, dst, ssem, rsem, to):
        return pltpu.make_async_remote_copy(src_ref=src, dst_ref=dst, send_sem=ssem, recv_sem=rsem, device_id=to, device_id_type=MESH)

    def copy_a(b):
        s = lax.rem(b, 2)
        return remote(part.at[s, 1 - core], ra.at[s], send_a.at[s], recv_a.at[s], sibling)

    def copy_b(b):
        s, r = lax.rem(b, 4), lax.rem(b, 8)
        return remote(sb.at[s], rb.at[r], send_b.at[s], recv_b.at[r], peer)

    def copy_c(b):
        r = lax.rem(b, 8)
        return remote(out.at[r, core, chip], out.at[r, core, chip], send_c.at[r], recv_c.at[r], peer)

    def copy_e(b):
        r = lax.rem(b, 8)
        return remote(out.at[r, core, chip], out.at[r, core, chip], send_e.at[r], recv_e.at[r], sibling)

    def copy_d(b):
        r = lax.rem(b, 8)
        return remote(out.at[r, core, 1 - chip], out.at[r, core, 1 - chip], send_d.at[r], recv_d.at[r], sibling)

    def copy_o(b):
        r = lax.rem(b, 8)
        return pltpu.make_async_copy(out.at[r], y_ref.at[b], osem.at[r])

    x_copy(0).start()
    w_copy(0).start()

    barrier = pltpu.get_barrier_semaphore()
    for other in (sibling, peer):
        pl.semaphore_signal(barrier, inc=1, device_id=other, device_id_type=MESH)
    pl.semaphore_wait(barrier, 2)

    for k in range(nx):
        if k + 1 < nx:
            x_copy(k + 1).start()
        x_copy(k).wait()

        def tile(t, carry, k=k):
            xp[pl.ds(pl.multiple_of(t * TILE, TILE), TILE), k * XC:(k + 1) * XC] = stages[k % 2][table_ref[t]]
            return carry

        lax.fori_loop(0, rows // TILE, tile, 0)

    def multiply(b, k):
        s = lax.rem(b, 2)
        prod = jnp.dot(xp[:, k * KC:(k + 1) * KC], wbuf[s, k * KC:(k + 1) * KC, :], preferred_element_type=jnp.float32)
        for h in range(2):
            piece = prod[:, h * HB:(h + 1) * HB]
            if k == 0:
                part[s, h] = piece
            else:
                part[s, h] = part[s, h] + piece

    def step(i, carry):
        @pl.when(i < blocks)
        def _():
            @pl.when(i + 1 < blocks)
            def _():
                w_copy(i + 1).start()

            w_copy(i).wait()
            for k in range(nk - 1):
                multiply(i, k)

        @pl.when(jnp.logical_and(i >= 1, i - 1 < blocks))
        def _():
            b = i - 1
            s, q = lax.rem(b, 2), lax.rem(b, 4)
            copy_a(b).wait()
            there = pl.ds(pl.multiple_of((1 - chip) * half, 8), half)
            here = pl.ds(pl.multiple_of(chip * half, 8), half)
            sb[q] = part[s, core, there, :] + ra[s, there, :]
            so[q] = part[s, core, here, :] + ra[s, here, :]
            copy_b(b).start()

        @pl.when(jnp.logical_and(i >= 3, i - 3 < blocks))
        def _():
            b = i - 3
            copy_b(b).wait()
            out[lax.rem(b, 8), core, chip] = (so[lax.rem(b, 4)] + rb[lax.rem(b, 8)]).astype(out.dtype)
            copy_c(b).start()
            copy_e(b).start()

        @pl.when(jnp.logical_and(i >= 5, i - 5 < blocks))
        def _():
            b = i - 5
            copy_c(b).wait()
            copy_d(b).start()

        @pl.when(jnp.logical_and(i >= 6, i - 6 < blocks))
        def _():
            b = i - 6
            copy_e(b).wait()
            copy_d(b).wait()
            copy_o(b).start()

        @pl.when(jnp.logical_and(i >= 7, i - 7 < blocks))
        def _():
            copy_o(i - 7).wait()

        @pl.when(i < blocks)
        def _():
            multiply(i, nk - 1)
            copy_a(i).start()

        return carry

    lax.fori_loop(0, blocks + LAST, step, 0)


def unpack_kernel(rows, per, lens_ref, p_ref, y_ref):
    slots = lens_ref.shape[0]
    tokens = y_ref.shape[0]
    slot_tiles = tokens // slots // TILE
    half = rows // 2
    offs, _ = tile_offsets(lens_ref, slots)
    for s in range(slots):
        def tile(t, carry, s=s):
            length = lens_ref[s]
            row = t * TILE + lax.broadcasted_iota(jnp.int32, (TILE, HB), 0)
            keep = row < length
            at = jnp.minimum(offs[s] + t, rows // TILE - 1)
            at = pl.multiple_of(at * TILE, TILE)
            target = pl.multiple_of((s * slot_tiles + t) * TILE, TILE)
            for j in range(per):
                for h in range(2):
                    piece = p_ref[j, h, pl.ds(at, TILE), :]
                    piece = jnp.where(keep, piece, jnp.zeros_like(piece))
                    y_ref[pl.ds(target, TILE), (2 * j + h) * HB:(2 * j + h + 1) * HB] = piece
            return carry

        lax.fori_loop(0, slot_tiles, tile, 0)


def branch(index, rows, x_loc, w_loc, lengths, table):
    tokens, depth = x_loc.shape
    cols = w_loc.shape[1]
    blocks = cols // NB
    half = rows // 2
    f32, bf16 = jnp.float32, x_loc.dtype
    dma = pltpu.SemaphoreType.DMA
    packed = pl.pallas_call(
        functools.partial(fused_kernel, rows),
        out_shape=jax.ShapeDtypeStruct((blocks, 2, 2, half, HB), bf16),
        in_specs=[pl.BlockSpec(memory_space=pltpu.SMEM), pl.BlockSpec(memory_space=pl.ANY), pl.BlockSpec(memory_space=pl.ANY)],
        out_specs=pl.BlockSpec(memory_space=pl.ANY),
        scratch_shapes=[
            pltpu.VMEM((rows, depth), bf16),
            pltpu.VMEM((tokens // TILE, TILE, XC), bf16),
            pltpu.VMEM((tokens // TILE, TILE, XC), bf16),
            pltpu.VMEM((2, depth, NB), bf16),
            pltpu.VMEM((2, 2, rows, HB), f32),
            pltpu.VMEM((2, rows, HB), f32),
            pltpu.VMEM((4, half, HB), f32),
            pltpu.VMEM((4, half, HB), f32),
            pltpu.VMEM((8, half, HB), f32),
            pltpu.VMEM((8, 2, 2, half, HB), bf16),
            dma((2,)), dma((2,)), dma((2,)), dma((2,)), dma((4,)), dma((8,)),
            dma((8,)), dma((8,)), dma((8,)), dma((8,)), dma((8,)), dma((8,)), dma((8,)),
        ],
        compiler_params=pltpu.CompilerParams(collective_id=index, has_side_effects=True, vmem_limit_bytes=66_000_000),
        cost_estimate=pl.CostEstimate(flops=2 * rows * depth * cols, bytes_accessed=2 * depth * cols, transcendentals=0),
        name=f"fused_{rows}",
    )(table, x_loc.reshape(tokens // TILE, TILE, depth), w_loc)
    packed = packed.reshape(blocks, 2, rows, HB)
    per = 4
    return pl.pallas_call(
        functools.partial(unpack_kernel, rows, per),
        out_shape=jax.ShapeDtypeStruct((tokens, cols), bf16),
        grid_spec=pltpu.PrefetchScalarGridSpec(
            num_scalar_prefetch=1,
            grid=(blocks // per,),
            in_specs=[pl.BlockSpec((per, 2, rows, HB), lambda g, lens: (g, 0, 0, 0))],
            out_specs=pl.BlockSpec((tokens, per * NB), lambda g, lens: (0, g)),
        ),
        cost_estimate=pl.CostEstimate(flops=0, bytes_accessed=2 * (rows + tokens) * cols, transcendentals=0),
        name=f"unpack_{rows}",
    )(lengths, packed)


def solution(mesh):
    def local_part(x_loc, w_loc, lengths):
        tokens, slots = x_loc.shape[0], lengths.shape[0]
        slot_tiles = tokens // slots // TILE
        tiles = (lengths + TILE - 1) // TILE
        ends = jnp.cumsum(tiles)
        place = jnp.arange(BUCKETS[-1] // TILE, dtype=jnp.int32)
        slot = jnp.minimum(jnp.sum((place[:, None] >= ends[None, :]).astype(jnp.int32), axis=1), slots - 1)
        first = jnp.sum(jnp.where(jnp.arange(slots)[None, :] < slot[:, None], tiles[None, :], 0), axis=1)
        table = slot * slot_tiles + jnp.minimum(place - first, slot_tiles - 1)
        index = jnp.sum((jnp.sum(tiles) * TILE > jnp.array(BUCKETS[:-1], jnp.int32)).astype(jnp.int32))
        return lax.switch(index, [functools.partial(branch, j, rows) for j, rows in enumerate(BUCKETS)], x_loc, w_loc, lengths, table)

    return jax.shard_map(local_part, mesh=mesh, in_specs=(P("data", "tp"), P("tp", None), P("data")), out_specs=P("data", None), check_vma=False)
```

time: 851 us -> 307 us (0.36)
  waiting for transfers between devices: 481 us -> 0 us
  matrix products: 326 us -> 0 us
  Pallas kernels: 0 us -> 302 us
  local copies, waits for them, and re-layouts: 21.5 us -> 0.01 us
  between operations: 13.4 us -> 1.31 us
    reduce_scatter x1 -> x0, waiting for transfers between devices: 328 us -> none  [local_part(): own_rows = lax.psum_scatter(part_sum, 'tp', scatter_dimension=0, tiled=True)]
    dot_general x1 -> x0, matrix products: 326 us -> none  [local_part(): part_sum = jnp.dot(x_loc, w_loc, preferred_element_type=jnp.float32)]
    pallas_call x0 -> x2, Pallas kernels: none -> 302 us  [the longest x1 280 us: branch(): pl.pallas_call(functools.partial(fused_kernel, rows), out_shape=jax.Shape...]
    all_gather x1 -> x0, waiting for transfers between devices: 153 us -> none  [local_part(): return lax.all_gather(own_out, 'tp', axis=0, tiled=True)]
    unnamed x3 -> x0, local copies, waits for them, and re-layouts: 21.4 us -> none
    convert_element_type x1 -> x0, other arithmetic: 8.56 us -> none  [local_part(): own_out = jnp.where(own_valid[:, None], own_rows, 0.0).astype(jnp.bfloat16)]
  transfers between devices with their start and end apart: 2 -> 0, of which waited for: 2 -> 0; matrix products, arithmetic and copies ran while one was open for 0% -> 0% of each run, Pallas kernels for 0% -> 0%
where the time goes in v1:
time: 307 us
  Pallas kernels  302 us (98%)
  other arithmetic  3.47 us (1%)
    pallas_call x1, Pallas kernels, branch(): pl.pallas_call(functools.partial(fused_kernel, rows), out_shape=jax.Shape...  280 us
    pallas_call x1, Pallas kernels, branch(): pl.pallas_call(functools.partial(unpack_kernel, rows, per), out_shape=jax...  21.8 us

profile of v1, /device:TPU:0, one launch (start us, length us, event | category | flops | bytes accessed | tf_op | source)
XLA Modules:
  0.0 306.7 jit_solution(14847179468178383685)
XLA Ops:
  0.0 1.3 fusion.9
  2.0 1.3 fusion.8
  3.9 0.2 reduce-window.8
  4.1 0.1 convert_reduce_fusion
  4.2 302.5 %conditional.1 = (bf16[1024,12288]{1,0:T(8,128)(2,1)}) conditional(s32[]{:T(128)} %clamp.3, (bf16[1024,12288]{1,0:T(8,128)(2,1)}, s32[49]{0:T(128)S(1)}, bf16[12288,12288]{1,0:T(8,128)(2,1)}, s32[4]{0:T(128)}, s32[49]{0:T(128)S(1)}, /*index=5*/s32[]{:T(128)}, s32[]{:T(128)}, s32[49,4]{0,1:T(4,128)S(1)}, s32[]{:T(128)}, ...), branch_computations={%region_5.6_spmd, %region_6.7_spmd, %region_7.8_spmd, %region_8.9_... | conditional | flops 236760072192 | bytes 346425376 | solution.py:243
  4.4 0.1 select_reduce_fusion.5
  4.5 0.5 fusion.5.table_ref
  5.0 0.0 copy-start.5
  5.0 279.9 %fused_640.1 = bf16[48,2,2,320,128]{4,3,2,1,0:T(8,128)(2,1)} custom-call(s32[49]{0:T(128)} %fusion.5.table_ref, bf16[64,16,12288]{2,1,0:T(8,128)(2,1)} %bitcast.32, bf16[12288,12288]{1,0:T(8,128)(2,1)} %get-tuple-element.188.w_ref), custom_call_target="tpu_custom_call" | custom-call | flops 193273528320 | bytes 301989888 | tf_op jit(solution)/shard_map/cond/branch_5_fun/fused_640/pallas_call | solution.py:193
  284.9 0.0 copy-done.5
  284.9 21.8 %unpack_640.1 = bf16[1024,12288]{1,0:T(8,128)(2,1)} custom-call(s32[4]{0:T(128)S(1)} %copy-done.5, bf16[48,2,640,128]{3,2,1,0:T(8,128)(2,1)} %bitcast.20), custom_call_target="tpu_custom_call" | custom-call | bytes 40894464 | tf_op jit(solution)/shard_map/cond/branch_5_fun/unpack_640/pallas_call | solution.py:218
  (3 shorter events, 0.0 us)
Async XLA Ops:
  5.0 279.9 %copy-start.5 = (s32[4]{0:T(128)S(1)}, s32[4]{0:T(128)}, u32[]{:S(2)}) copy-start(s32[4]{0:T(128)} %get-tuple-element.98.lens_ref) | copy-start | bytes 52 | tf_op jit(solution)/shard_map/cond
